TPU v7x, 32 devices: a whole 2x2x4 slice. The times are simulated.
32 devices in a mesh: space: 8 (over y, x, core), tm: 4 (over z).
Axes of the slice: x: 2, y: 2, z: 4, core: 2. Of those that a mesh axis runs over, the one named last changes fastest.
Arguments:
- vectors: bfloat16 [4, 2, 3, 96, 4096], P('tm', None, None, None, 'space'), may hold values from -6 to 6
- momenta: int32 [2, 3], replicated, may hold values from -3 to 3
- offsets: int32 [8, 3], replicated, may hold values from 0 to 56, as said below
Outputs:
- elementals: float32 [4, 96, 2, 18432], P(None, 'space')
Inputs may be any that keep to these rules, and one draw needn't show every extreme that they name: `offsets`: each row is the corner of one block of 8 x 8 x 8 sites of the 64^3 lattice: its first two coordinates are multiples of 8, its third a multiple of 8; no two rows name the same block, so the blocks never intersect.
All inputs are finite; a program needn't handle non-finite values.
Results may differ from a plain program's by a relative error of at most 0.0055.
Values may be sent and summed in bfloat16 or wider, within the bound.
A program may use at most 128 MiB of HBM per device.

v0:
```python
import functools
import math

import jax
import jax.numpy as jnp
from jax import lax
from jax.experimental import pallas as pl
from jax.experimental.pallas import tpu as pltpu
from jax.sharding import PartitionSpec as P

LAT = 64
BRICK = 8
BRICK_Z = 8
JB = 32
LANES = 128


def local_coords(site):
    return jnp.stack([site // (BRICK * BRICK_Z), site // BRICK_Z % BRICK, site % BRICK_Z])


def phases(momenta, coords):
    product = jnp.sum(momenta[:, :, None] * coords[None, :, :], axis=1)
    angle = (product % LAT).astype(jnp.float32) * (2.0 * math.pi / LAT)
    return jnp.stack([jnp.cos(angle), jnp.sin(angle)], axis=1)


def compute_kernel(scale, first, seeded, v_ref, row_ref, phase_ref, *refs):
    nvec = v_ref.shape[3]
    sites = v_ref.shape[4]
    rows = row_ref.shape[3]
    moments = phase_ref.shape[1] // 2
    nblocks = nvec // JB
    group = 2 * moments * JB
    if seeded:
        seed_ref, out_ref, row_f, vp_ref = refs[0], refs[1], refs[2], refs[3]
        rest = refs[4:]
        count = len(rest) // 2
        lhs_refs, acc_refs = rest[:count], rest[count:]
    else:
        acc_out, row_f, vp_ref = refs[0], refs[1], refs[2]
        lhs_refs = refs[3:]
        count = len(lhs_refs)
        starts = []
        at = 0
        for n in range(count):
            starts.append(at)
            at += (nblocks - first - n) * group
        acc_refs = [
            acc_out.at[:, pl.ds(starts[n], (nblocks - first - n) * group)] for n in range(count)
        ]
    step = pl.program_id(0)

    @pl.when(step == 0)
    def _():
        at = 0
        for acc in acc_refs:
            wide = acc.shape[1]
            if seeded:
                acc[...] = seed_ref[:, at : at + wide]
            else:
                acc[...] = jnp.zeros(acc.shape, jnp.float32)
            at += wide

    for q in range(2):
        for colour in range(3):
            row_f[q * 3 + colour] = row_ref[0, q, colour].astype(jnp.float32)

    def chunk(index, carry):
        lanes = pl.ds(pl.multiple_of(index * LANES, LANES), LANES)
        for colour in range(3):
            real_v = v_ref[0, 0, colour, :, lanes].astype(jnp.float32)
            imag_v = v_ref[0, 1, colour, :, lanes].astype(jnp.float32)
            for p in range(moments):
                cosine = phase_ref[0, pl.ds(2 * p, 1), lanes]
                sine = phase_ref[0, pl.ds(2 * p + 1, 1), lanes]
                real_x = (cosine * real_v - sine * imag_v).astype(jnp.bfloat16)
                imag_x = (cosine * imag_v + sine * real_v).astype(jnp.bfloat16)
                table = ((real_x, -imag_x), (imag_x, real_x))
                for r in range(2):
                    for q in range(2):
                        at = (colour * 2 + q) * LANES
                        for kb in range(first, nblocks):
                            base = (kb - first) * group + (2 * p + r) * JB
                            vp_ref[base : base + JB, at : at + LANES] = table[r][q][
                                kb * JB : (kb + 1) * JB
                            ]
        for n in range(count):
            jb = first + n
            vecs = [
                [v_ref[0, q, colour, jb * JB : (jb + 1) * JB, lanes] for colour in range(3)]
                for q in range(2)
            ]
            for i in range(rows):
                row = [
                    [
                        jnp.broadcast_to(
                            row_f[q * 3 + colour, pl.ds(i, 1), lanes], (JB, LANES)
                        ).astype(jnp.bfloat16)
                        for colour in range(3)
                    ]
                    for q in range(2)
                ]
                for colour in range(3):
                    a = (colour + 1) % 3
                    b = (colour + 2) % 3
                    real_d = (row[0][a] * vecs[0][b] - row[1][a] * vecs[1][b]) - (
                        row[0][b] * vecs[0][a] - row[1][b] * vecs[1][a]
                    )
                    imag_d = (row[0][a] * vecs[1][b] + row[1][a] * vecs[0][b]) - (
                        row[0][b] * vecs[1][a] + row[1][b] * vecs[0][a]
                    )
                    at = colour * 2 * LANES
                    lhs_refs[n][i * JB : (i + 1) * JB, at : at + LANES] = real_d
                    lhs_refs[n][i * JB : (i + 1) * JB, at + LANES : at + 2 * LANES] = imag_d
            acc_refs[n][...] += lax.dot_general(
                lhs_refs[n][...],
                vp_ref[n * group :, :],
                (((1,), (1,)), ((), ())),
                preferred_element_type=jnp.float32,
            )
        return carry

    lax.fori_loop(0, sites // LANES, chunk, 0)

    if seeded:

        @pl.when(step == pl.num_programs(0) - 1)
        def _():
            at = 0
            for acc in acc_refs:
                wide = acc.shape[1]
                out_ref[:, at : at + wide] = (acc[...] * scale).astype(jnp.bfloat16)
                at += wide


def contract(gathered, row_vecs, phase, scale, first, last, seed, seed_block):
    groups, _, _, nvec, sites = gathered.shape
    rows = row_vecs.shape[3]
    moments = phase.shape[1] // 2
    nblocks = nvec // JB
    group = 2 * moments * JB
    widths = [(nblocks - jb) * group for jb in range(first, last)]
    total = sum(widths)
    depth = 6 * LANES
    seeded = seed is not None
    in_specs = [
        pl.BlockSpec((1, 2, 3, nvec, sites), lambda s: (s, 0, 0, 0, 0)),
        pl.BlockSpec((1, 2, 3, rows, sites), lambda s: (s, 0, 0, 0, 0)),
        pl.BlockSpec((1, 2 * moments, sites), lambda s: (s, 0, 0)),
    ]
    operands = [gathered, row_vecs, phase]
    scratch = [
        pltpu.VMEM((6, rows, sites), jnp.float32),
        pltpu.VMEM((widths[0], depth), jnp.bfloat16),
    ] + [pltpu.VMEM((rows * JB, depth), jnp.bfloat16) for _ in widths]
    if seeded:
        in_specs.append(pl.BlockSpec((rows * JB, total), lambda s: (0, seed_block)))
        operands.append(seed)
        scratch += [pltpu.VMEM((rows * JB, wide), jnp.float32) for wide in widths]
    return pl.pallas_call(
        functools.partial(compute_kernel, scale, first, seeded),
        out_shape=jax.ShapeDtypeStruct(
            (rows * JB, total), jnp.bfloat16 if seeded else jnp.float32
        ),
        grid=(groups,),
        in_specs=in_specs,
        out_specs=pl.BlockSpec((rows * JB, total), lambda s: (0, 0)),
        scratch_shapes=scratch,
        compiler_params=pltpu.CompilerParams(dimension_semantics=("arbitrary",)),
        cost_estimate=pl.CostEstimate(
            flops=2 * groups * sites * 6 * rows * JB * total * 2,
            bytes_accessed=groups * 6 * nvec * sites * 2,
            transcendentals=0,
        ),
        name="contract",
    )(*operands)


def unpack_kernel(rows, moments, nvec, *refs):
    nblocks = nvec // JB
    group = 2 * moments * JB
    pack = LANES // JB
    head_ref, tail_ref, out_ref, full = refs
    tall = full.shape[0] // (rows * moments)
    pieces = []
    for n in range(nblocks):
        source = head_ref if n == 0 else tail_ref
        at = 0 if n == 0 else sum((nblocks - m) * group for m in range(1, n))
        for kb in range(n, nblocks):
            pieces.append((n, kb, source, at))
            at += group
    for jb, kb, source, at in pieces:
        for start in range(0, rows, pack):
            many = min(pack, rows - start)
            block = source[0, start * JB : (start + many) * JB, at : at + group].astype(
                jnp.float32
            )
            turned = -jnp.transpose(block) if jb != kb else None
            for n in range(many):
                for p in range(moments):
                    which = (start + n) * moments + p
                    for r in range(2):
                        lane = (2 * p + r) * JB
                        tile, spot = divmod(r * nvec + kb * JB, LANES)
                        full[
                            which * tall + tile, jb * JB : (jb + 1) * JB, spot : spot + JB
                        ] = block[n * JB : (n + 1) * JB, lane : lane + JB]
                        if jb != kb:
                            tile, spot = divmod(r * nvec + jb * JB, LANES)
                            full[
                                which * tall + tile, kb * JB : (kb + 1) * JB, spot : spot + JB
                            ] = turned[lane : lane + JB, n * JB : (n + 1) * JB]
    wide = 2 * nvec
    tiles = 2 * wide // LANES
    half = nvec // 2
    for which in range(rows * moments):
        parity = []
        for odd in range(2):
            for tile in range(tall):
                line = full[which * tall + tile, pl.ds(odd, half, stride=2), :]
                parity.append(line[:, : min(LANES, wide - tile * LANES)])
        both = jnp.concatenate(parity, axis=1)
        i, p = which // moments, which % moments
        base = i * half * tiles * moments
        for tile in range(tiles):
            out_ref[0, pl.ds(base + tile * moments + p, half, stride=tiles * moments), :] = both[
                :, tile * LANES : (tile + 1) * LANES
            ]


def unpack(head, tail, rows, moments, nvec):
    times = head.shape[0]
    lines = nvec * nvec * 2 // LANES
    flat = pl.pallas_call(
        functools.partial(unpack_kernel, rows, moments, nvec),
        out_shape=jax.ShapeDtypeStruct((times, rows * lines * moments, LANES), jnp.float32),
        grid=(times,),
        in_specs=[
            pl.BlockSpec((1,) + head.shape[1:], lambda t: (t, 0, 0)),
            pl.BlockSpec((1,) + tail.shape[1:], lambda t: (t, 0, 0)),
        ],
        out_specs=pl.BlockSpec((1, rows * lines * moments, LANES), lambda t: (t, 0, 0)),
        scratch_shapes=[
            pltpu.VMEM((rows * moments * -(-2 * nvec // LANES), nvec, LANES), jnp.float32)
        ],
        compiler_params=pltpu.CompilerParams(dimension_semantics=("arbitrary",)),
        name="unpack",
    )(head, tail)
    flat = flat.reshape(times, rows, lines, moments, LANES)
    return jnp.transpose(flat, (0, 1, 3, 2, 4)).reshape(times, rows, moments, lines * LANES)


def body(vectors, momenta, offsets):
    local = vectors[0]
    nvec = local.shape[2]
    sites = local.shape[3]
    groups = lax.axis_size("space")
    rows = nvec // groups
    moments = momenta.shape[0]
    nblocks = nvec // JB
    group = 2 * moments * JB
    mine = lax.axis_index("space") * rows
    half = sites // 2
    site_ids = jnp.arange(sites, dtype=jnp.int32)
    coords = local_coords(site_ids)[:, None, :] + jnp.transpose(offsets)[:, :, None]
    phase = phases(momenta, coords.reshape(3, groups * sites))
    phase = jnp.transpose(phase.reshape(2 * moments, groups, sites), (1, 0, 2))
    scale = 1.0 / math.sqrt(sites * groups)
    early = lax.all_gather(local[..., :half], "space", axis=0)
    late = lax.all_gather(local[..., half:], "space", axis=0)
    early_rows = lax.dynamic_slice_in_dim(early, mine, rows, 3)
    partial = contract(early, early_rows, phase[..., :half], scale, 0, nblocks, None, 0)
    late, partial = lax.optimization_barrier((late, partial))
    late_rows = lax.dynamic_slice_in_dim(late, mine, rows, 3)
    stage = (late, late_rows, phase[..., half:])
    cut = nblocks * group
    seeds = [(partial, 0), (partial, 1)]
    if 2 * cut != partial.shape[1]:
        seeds = [(partial[:, :cut], 0), (partial[:, cut:], 0)]
    head = contract(*stage, scale, 0, 1, *seeds[0])
    head = lax.all_gather(head, "tm", axis=0)
    tail = contract(*stage, scale, 1, nblocks, *seeds[1])
    tail = lax.all_gather(tail, "tm", axis=0)
    return unpack(head, tail, rows, moments, nvec)


def solution(mesh):
    return jax.shard_map(
        body,
        mesh=mesh,
        in_specs=(P("tm", None, None, None, "space"), P(), P()),
        out_specs=P(None, "space", None, None),
        check_vma=False,
    )
```

profile of v0, /device:TPU:0, one launch (start us, length us, event | category | flops | bytes accessed | tf_op | source)
XLA Modules:
  0.0 161.1 jit_solution(8468818117489288448)
XLA Ops:
  6.5 0.0 all-gather.11.cloned.1.call-start
  6.5 1.9 %fusion.6 = (bf16[2,3,96,256]{3,2,1,0:T(8,128)(2,1)}, bf16[2,3,96,256]{3,2,1,0:T(8,128)(2,1)}) fusion(bf16[2,3,96,512]{3,2,1,0:T(8,128)(2,1)} %bitcast.25), kind=kLoop, calls=%fused_computation.27 | loop fusion | bytes 1179648 | tf_op jit(solution)/shard_map/slice | solution.py:270
  8.4 0.0 all-gather.11.cloned.1.call-update
  8.5 0.0 all-gather.9.cloned.1.call-start
  8.5 0.7 all-gather.9.cloned.1.call-update
  9.2 0.0 all-gather.13.cloned.1.call-start
  9.3 0.8 copy.9
  10.1 0.8 add_bitcast_fusion
  10.9 0.1 multiply_reduce_fusion
  11.0 0.5 fusion.4
  11.6 0.1 copy.10
  11.6 0.1 reshape.187
  11.7 0.6 fusion.7
  12.4 28.5 %all-gather.11.cloned.1.call-done = bf16[16,3,96,256]{3,2,1,0:T(8,128)(2,1)} async-done(((bf16[2,3,96,256]{3,2,1,0:T(8,128)(2,1)}), bf16[16,3,96,256]{3,2,1,0:T(8,128)(2,1)}) %all-gather.11.cloned.1.call-update) | async-done | bytes 2359312 | tf_op jit(solution)/shard_map/all_gather | solution.py:270
  40.9 2.0 %constant_dynamic-slice_fusion.1.row_ref = bf16[8,2,3,12,256]{4,3,2,1,0:T(8,128)(2,1)} fusion(bf16[8,2,3,96,256]{4,3,2,1,0:T(8,128)(2,1)} %bitcast.31, s32[]{:T(128)S(6)} %select_n.68), kind=kLoop, calls=%fused_computation.26 | loop fusion | bytes 589828 | tf_op jit(solution)/shard_map/dynamic_slice | solution.py:272
  42.8 19.1 %contract.3.refs_0_ = f32[384,768]{1,0:T(8,128)} custom-call(bf16[8,2,3,96,256]{4,3,2,1,0:T(8,128)(2,1)} %bitcast.32, bf16[8,2,3,12,256]{4,3,2,1,0:T(8,128)(2,1)} %constant_dynamic-slice_fusion.1.row_ref, f32[8,4,256]{2,1,0:T(4,128)} %get-tuple-element.12.phase_ref), custom_call_target="tpu_custom_call" | custom-call | flops 14495514624 | bytes 2359296 | tf_op jit(solution)/shard_map/contract/pallas_call | solution.py:161
  62.0 9.7 %all-gather.9.cloned.1.call-done = bf16[16,3,96,256]{3,2,1,0:T(8,128)(2,1)} async-done(((bf16[2,3,96,256]{3,2,1,0:T(8,128)(2,1)}), bf16[16,3,96,256]{3,2,1,0:T(8,128)(2,1)}) %all-gather.9.cloned.1.call-update) | async-done | bytes 2359312 | tf_op jit(solution)/shard_map/all_gather | solution.py:271
  71.7 2.0 %constant_dynamic-slice_fusion.row_ref = bf16[8,2,3,12,256]{4,3,2,1,0:T(8,128)(2,1)} fusion(bf16[8,2,3,96,256]{4,3,2,1,0:T(8,128)(2,1)} %bitcast.28, s32[]{:T(128)S(6)} %select_n.68), kind=kLoop, calls=%fused_computation.25 | loop fusion | bytes 589828 | tf_op jit(solution)/shard_map/dynamic_slice | solution.py:275
  73.6 11.6 %contract.4 = bf16[384,384]{1,0:T(8,128)(2,1)} custom-call(bf16[8,2,3,96,256]{4,3,2,1,0:T(8,128)(2,1)} %bitcast.29, bf16[8,2,3,12,256]{4,3,2,1,0:T(8,128)(2,1)} %constant_dynamic-slice_fusion.row_ref, f32[8,4,256]{2,1,0:T(4,128)} %get-tuple-element.11.phase_ref, f32[384,768]{1,0:T(8,128)} %contract.3.refs_0_), custom_call_target="tpu_custom_call" | custom-call | flops 7247757312 | bytes 2359296 | tf_op jit(solution)/shard_map/contract/pallas_call | solution.py:161
  85.2 0.0 all-gather.13.cloned.1.call-update
  85.2 0.0 all-gather.15.cloned.1.call-start
  85.3 14.7 %contract.5 = bf16[384,384]{1,0:T(8,128)(2,1)} custom-call(bf16[8,2,3,96,256]{4,3,2,1,0:T(8,128)(2,1)} %bitcast.30, bf16[8,2,3,12,256]{4,3,2,1,0:T(8,128)(2,1)} %constant_dynamic-slice_fusion.row_ref, f32[8,4,256]{2,1,0:T(4,128)} %get-tuple-element.11.phase_ref, f32[384,768]{1,0:T(8,128)} %contract.3.refs_0_), custom_call_target="tpu_custom_call" | custom-call | flops 7247757312 | bytes 2359296 | tf_op jit(solution)/shard_map/contract/pallas_call | solution.py:161
  100.0 0.0 all-gather.15.cloned.1.call-update
  100.0 15.6 %all-gather.13.cloned.1.call-done = bf16[1536,384]{1,0:T(8,128)(2,1)} async-done(((bf16[384,384]{1,0:T(8,128)(2,1)}), bf16[1536,384]{1,0:T(8,128)(2,1)}) %all-gather.13.cloned.1.call-update) | async-done | bytes 1179664 | tf_op jit(solution)/shard_map/all_gather | solution.py:282
  115.7 30.9 %all-gather.15.cloned.1.call-done = bf16[1536,384]{1,0:T(8,128)(2,1)} async-done(((bf16[384,384]{1,0:T(8,128)(2,1)}), bf16[1536,384]{1,0:T(8,128)(2,1)}) %all-gather.15.cloned.1.call-update) | async-done | bytes 1179664 | tf_op jit(solution)/shard_map/all_gather | solution.py:284
  146.6 8.0 %unpack.1 = f32[4,3456,128]{2,1,0:T(8,128)} custom-call(bf16[4,384,384]{2,1,0:T(8,128)(2,1)} %bitcast.23, bf16[4,384,384]{2,1,0:T(8,128)(2,1)} %bitcast.24), custom_call_target="tpu_custom_call" | custom-call | tf_op jit(solution)/shard_map/unpack/pallas_call | solution.py:235
  (6 shorter events, 0.1 us)
Async XLA Ops:
  6.5 34.3 %all-gather.11.cloned.1.call-start = ((), (), s32[]{:S(2)}) async-start(), calls=%async_computation.1 | async-start | bytes 2654208 | tf_op jit(solution)/shard_map/all_gather | solution.py:270
  8.5 63.2 %all-gather.9.cloned.1.call-start = ((), (), s32[]{:S(2)}) async-start(), calls=%async_computation | async-start | bytes 2654208 | tf_op jit(solution)/shard_map/all_gather | solution.py:271
  9.2 106.4 %all-gather.13.cloned.1.call-start = ((), (), s32[]{:S(2)}) async-start(), calls=%async_computation.2 | async-start | bytes 1474560 | tf_op jit(solution)/shard_map/all_gather | solution.py:282
  85.2 61.4 %all-gather.15.cloned.1.call-start = ((), (), s32[]{:S(2)}) async-start(), calls=%async_computation.3 | async-start | bytes 1474560 | tf_op jit(solution)/shard_map/all_gather | solution.py:284
Sparse Core Ops, SparseCore 0:
  9.2 31.5 all-gather.10
  42.7 28.8 all-gather.8
  85.4 30.2 all-gather.12
  117.1 29.4 all-gather.14
where the time goes:
time: 162 us; the launch traced here: 161 us
  waiting for transfers between devices  85.5 us (53%)
  Pallas kernels  53.4 us (33%)
  between operations  13.2 us (8%)
  local copies, waits for them, and re-layouts  7.46 us (5%)
    pallas_call x3, Pallas kernels, contract(): pl.pallas_call(functools.partial(compute_kernel, scale, first, seeded), o...  45.4 us
    all_gather x1, waiting for transfers between devices, body(): tail = lax.all_gather(tail, 'tm', axis=0)  30.9 us
    all_gather x1, waiting for transfers between devices, body(): early = lax.all_gather(local[..., :half], 'space', axis=0)  28.5 us
    all_gather x1, waiting for transfers between devices, body(): head = lax.all_gather(head, 'tm', axis=0)  15.6 us
    all_gather x1, waiting for transfers between devices, body(): late = lax.all_gather(local[..., half:], 'space', axis=0)  9.66 us
    pallas_call x1, Pallas kernels, unpack(): pl.pallas_call(functools.partial(unpack_kernel, rows, moments, nvec), out...  8 us
  transfers between devices with their start and end apart: 4, of which 4 were waited for; matrix products, arithmetic and copies ran while one was open for 3% of the time, Pallas kernels for 21%

commit v1 on v0

v1 whole, which is shorter than its diff:
```python
import functools
import math

import jax
import jax.numpy as jnp
from jax import lax
from jax.experimental import pallas as pl
from jax.experimental.pallas import tpu as pltpu
from jax.sharding import PartitionSpec as P

LAT = 64
BRICK = 8
BRICK_Z = 8
JB = 32
LANES = 128


MESH = pl.DeviceIdType.MESH


def fill_phase(phase_ref, half, block, mom_ref, off_ref):
    sites = phase_ref.shape[2]
    moments = mom_ref.shape[0]
    site = lax.broadcasted_iota(jnp.int32, (1, sites), 1)
    coords = [site // (BRICK * BRICK_Z), site // BRICK_Z % BRICK, site % BRICK_Z]
    for p in range(moments):
        product = jnp.zeros((1, sites), jnp.int32)
        for axis in range(3):
            product = product + mom_ref[p, axis] * (coords[axis] + off_ref[block, axis])
        angle = (product % LAT).astype(jnp.float32) * (2.0 * math.pi / LAT)
        phase_ref[half, 2 * p : 2 * p + 1, :] = jnp.cos(angle)
        phase_ref[half, 2 * p + 1 : 2 * p + 2, :] = jnp.sin(angle)


def elementals_kernel(
    scale,
    chips,
    times,
    rows,
    mom_ref,
    off_ref,
    v_ref,
    z_ref,
    other_ref,
    phase_ref,
    rowf_ref,
    x_ref,
    lhs_a,
    lhs_b,
    acc_ref,
    own_ref,
    send_ref,
    take_ref,
    fin_ref,
    pair_sem,
    send_sem,
    take_sem,
    fin_sem,
    z_sem,
    up_sem,
    down_sem,
):
    nvec = v_ref.shape[2]
    sites = v_ref.shape[3]
    moments = mom_ref.shape[0]
    nblocks = nvec // JB
    group = 2 * moments * JB
    per_half = sites // LANES
    nchunks = 2 * per_half
    depth = 6 * LANES
    me = lax.axis_index("space")
    z = lax.axis_index("tm")
    core = lax.rem(me, 2)
    chip = me // 2
    mate = chip * 2 + 1 - core
    first = [sum((nblocks - m) * group for m in range(jb)) for jb in range(nblocks)]
    width = [(nblocks - jb) * group for jb in range(nblocks)]

    barrier = pltpu.get_barrier_semaphore()

    def greet(where):
        pl.semaphore_signal(barrier, inc=1, device_id=where, device_id_type=MESH)

    greet({"space": mate})
    for s in range(1, chips):
        greet({"space": lax.rem(chip + s, chips) * 2 + core})

    @pl.when(z > 0)
    def _():
        greet({"tm": z - 1})

    @pl.when(z < times - 1)
    def _():
        greet({"tm": z + 1})

    ends = jnp.minimum(z, 1) + jnp.minimum(times - 1 - z, 1)
    pl.semaphore_wait(barrier, chips + ends)

    pair = pltpu.make_async_remote_copy(
        src_ref=v_ref,
        dst_ref=other_ref,
        send_sem=pair_sem.at[0],
        recv_sem=pair_sem.at[1],
        device_id={"space": mate},
        device_id_type=MESH,
    )
    pair.start()
    fill_phase(phase_ref, 0, me, mom_ref, off_ref)
    fill_phase(phase_ref, 1, mate, mom_ref, off_ref)

    def prepare(half, source):
        def one(index, carry):
            lanes = pl.ds(pl.multiple_of(index * LANES, LANES), LANES)
            chunk = half * per_half + index
            for colour in range(3):
                real_v = source[0, colour, :, lanes].astype(jnp.float32)
                imag_v = source[1, colour, :, lanes].astype(jnp.float32)
                rowf_ref[chunk, colour] = real_v
                rowf_ref[chunk, 3 + colour] = imag_v
                for p in range(moments):
                    cosine = phase_ref[half, pl.ds(2 * p, 1), lanes]
                    sine = phase_ref[half, pl.ds(2 * p + 1, 1), lanes]
                    real_x = (cosine * real_v - sine * imag_v).astype(jnp.bfloat16)
                    imag_x = (cosine * imag_v + sine * real_v).astype(jnp.bfloat16)
                    table = ((real_x, -imag_x), (imag_x, real_x))
                    for r in range(2):
                        for part in range(2):
                            at = (colour * 2 + part) * LANES
                            for kb in range(nblocks):
                                base = kb * group + (2 * p + r) * JB
                                x_ref[chunk, base : base + JB, at : at + LANES] = table[r][part][
                                    kb * JB : (kb + 1) * JB
                                ]
            return carry

        lax.fori_loop(0, per_half, one, 0)

    prepare(0, v_ref)
    pair.wait()
    prepare(1, other_ref)

    def form(lhs, chunk, jb, row0):
        vecs = [
            [
                rowf_ref[chunk, part * 3 + colour, jb * JB : (jb + 1) * JB, :].astype(jnp.bfloat16)
                for colour in range(3)
            ]
            for part in range(2)
        ]
        for i in range(rows):
            row = [
                [
                    jnp.broadcast_to(
                        rowf_ref[chunk, part * 3 + colour, pl.ds(row0 + i, 1), :], (JB, LANES)
                    ).astype(jnp.bfloat16)
                    for colour in range(3)
                ]
                for part in range(2)
            ]
            for colour in range(3):
                a = (colour + 1) % 3
                b = (colour + 2) % 3
                real_d = (row[0][a] * vecs[0][b] - row[1][a] * vecs[1][b]) - (
                    row[0][b] * vecs[0][a] - row[1][b] * vecs[1][a]
                )
                imag_d = (row[0][a] * vecs[1][b] + row[1][a] * vecs[0][b]) - (
                    row[0][b] * vecs[1][a] + row[1][b] * vecs[0][a]
                )
                at = colour * 2 * LANES
                lhs[i * JB : (i + 1) * JB, at : at + LANES] = real_d
                lhs[i * JB : (i + 1) * JB, at + LANES : at + 2 * LANES] = imag_d

    def product(lhs, chunk, jb):
        return lax.dot_general(
            lhs[...],
            x_ref[chunk, jb * group :, :],
            (((1,), (1,)), ((), ())),
            preferred_element_type=jnp.float32,
        )

    def target(s):
        return lax.rem(chip + s + 1, chips)

    def forward(s, jb):
        cols = pl.ds(first[jb], width[jb])
        return pltpu.make_async_remote_copy(
            src_ref=send_ref.at[s, :, cols],
            dst_ref=take_ref.at[s, :, cols],
            send_sem=send_sem.at[jb, s],
            recv_sem=take_sem.at[jb, s],
            device_id={"space": target(s) * 2 + core},
            device_id_type=MESH,
        )

    def climb(t, jb):
        cols = pl.ds(first[jb], width[jb])
        return pltpu.make_async_remote_copy(
            src_ref=z_ref.at[t, :, cols],
            dst_ref=z_ref.at[t, :, cols],
            send_sem=up_sem.at[jb, t],
            recv_sem=z_sem.at[jb, t],
            device_id={"tm": z + 1},
            device_id_type=MESH,
        )

    def descend(t, jb):
        cols = pl.ds(first[jb], width[jb])
        return pltpu.make_async_remote_copy(
            src_ref=z_ref.at[t, :, cols],
            dst_ref=z_ref.at[t, :, cols],
            send_sem=down_sem.at[jb, t],
            recv_sem=z_sem.at[jb, t],
            device_id={"tm": z - 1},
            device_id_type=MESH,
        )

    def finish(jb):
        lo, hi = first[jb], first[jb] + width[jb]
        total = own_ref[:, lo:hi]
        for s in range(chips - 1):
            forward(s, jb).wait_recv()
            total = total + take_ref[s, :, lo:hi].astype(jnp.float32)
        z_ref[z, :, lo:hi] = (total * scale).astype(jnp.bfloat16)

        @pl.when(z < times - 1)
        def _():
            climb(z, jb).start()

        @pl.when(z > 0)
        def _():
            descend(z, jb).start()

    def relay(jb, dist):
        @pl.when(z - dist >= 0)
        def _():
            descend(z - dist, jb).wait_recv()

            @pl.when(z < times - 1)
            def _():
                climb(z - dist, jb).start()

        @pl.when(z + dist < times)
        def _():
            climb(z + dist, jb).wait_recv()

            @pl.when(z > 0)
            def _():
                descend(z + dist, jb).start()

    def run(jb, after):
        lo, hi = first[jb], first[jb] + width[jb]
        wide = width[jb]

        def one(s, carry):
            row0 = (target(s) * 2 + core) * rows
            form(lhs_a, 0, jb, row0)
            acc_ref[:, :wide] = jnp.zeros((rows * JB, wide), jnp.float32)

            def two(m, carry):
                form(lhs_b, 2 * m + 1, jb, row0)
                acc_ref[:, :wide] += product(lhs_a, 2 * m, jb)
                form(lhs_a, lax.rem(2 * m + 2, nchunks), jb, row0)
                acc_ref[:, :wide] += product(lhs_b, 2 * m + 1, jb)
                return carry

            lax.fori_loop(0, nchunks // 2, two, 0)

            @pl.when(s < chips - 1)
            def _():
                send_ref[s, :, lo:hi] = acc_ref[:, :wide].astype(jnp.bfloat16)
                forward(s, jb).start()

            @pl.when(s == chips - 1)
            def _():
                own_ref[:, lo:hi] = acc_ref[:, :wide]

            for when, act in after:

                @pl.when(s == when)
                def _():
                    act()

            return carry

        lax.fori_loop(0, chips, one, 0)

    order = list(range(nblocks - 1, -1, -1))
    for n, jb in enumerate(order):
        after = []
        if n >= 1:
            after.append((0, functools.partial(finish, order[n - 1])))
        if n >= 2:
            after.append((chips // 2, functools.partial(relay, order[n - 2], 1)))
        run(jb, after)
    for dist in range(2, times):
        for jb in order[:-2]:
            relay(jb, dist)
    if nblocks > 1:
        relay(order[-2], 1)
    finish(order[-1])
    if nblocks > 1:
        for dist in range(2, times):
            relay(order[-2], dist)
    for dist in range(1, times):
        relay(order[-1], dist)

    for jb in range(nblocks):
        for s in range(chips - 1):
            forward(s, jb).wait_send()
        for t in range(times):

            @pl.when((z < times - 1) & (t <= z))
            def _():
                climb(t, jb).wait_send()

            @pl.when((z > 0) & (t >= z))
            def _():
                descend(t, jb).wait_send()


def elementals(local, momenta, offsets):
    nvec = local.shape[2]
    sites = local.shape[3]
    groups = lax.axis_size("space")
    times = lax.axis_size("tm")
    chips = groups // 2
    rows = nvec // groups
    moments = momenta.shape[0]
    nblocks = nvec // JB
    group = 2 * moments * JB
    total = sum((nblocks - jb) * group for jb in range(nblocks))
    nchunks = 2 * sites // LANES
    depth = 6 * LANES
    tall = rows * JB
    scale = 1.0 / math.sqrt(sites * groups)
    dma = pltpu.SemaphoreType.DMA
    return pl.pallas_call(
        functools.partial(elementals_kernel, scale, chips, times, rows),
        out_shape=jax.ShapeDtypeStruct((times, tall, total), jnp.bfloat16),
        in_specs=[
            pl.BlockSpec(memory_space=pltpu.SMEM),
            pl.BlockSpec(memory_space=pltpu.SMEM),
            pl.BlockSpec(memory_space=pltpu.VMEM),
        ],
        out_specs=pl.BlockSpec(memory_space=pltpu.VMEM),
        scratch_shapes=[
            pltpu.VMEM((2, 3, nvec, sites), jnp.bfloat16),
            pltpu.VMEM((2, 2 * moments, sites), jnp.float32),
            pltpu.VMEM((nchunks, 6, nvec, LANES), jnp.float32),
            pltpu.VMEM((nchunks, nblocks * group, depth), jnp.bfloat16),
            pltpu.VMEM((tall, depth), jnp.bfloat16),
            pltpu.VMEM((tall, depth), jnp.bfloat16),
            pltpu.VMEM((tall, nblocks * group), jnp.float32),
            pltpu.VMEM((tall, total), jnp.float32),
            pltpu.VMEM((chips - 1, tall, total), jnp.bfloat16),
            pltpu.VMEM((chips - 1, tall, total), jnp.bfloat16),
            pltpu.VMEM((8, LANES), jnp.float32),
            dma((2,)),
            dma((nblocks, chips - 1)),
            dma((nblocks, chips - 1)),
            dma((2,)),
            dma((nblocks, times)),
            dma((nblocks, times)),
            dma((nblocks, times)),
        ],
        compiler_params=pltpu.CompilerParams(
            collective_id=0, has_side_effects=True, vmem_limit_bytes=60 * 1024 * 1024
        ),
        name="elementals",
    )(momenta, offsets, local)


def unpack_kernel(rows, moments, nvec, *refs):
    nblocks = nvec // JB
    group = 2 * moments * JB
    pack = LANES // JB
    source, out_ref, full = refs
    tall = full.shape[0] // (rows * moments)
    pieces = []
    at = 0
    for n in range(nblocks):
        for kb in range(n, nblocks):
            pieces.append((n, kb, at))
            at += group
    for jb, kb, at in pieces:
        for start in range(0, rows, pack):
            many = min(pack, rows - start)
            block = source[0, start * JB : (start + many) * JB, at : at + group].astype(
                jnp.float32
            )
            turned = -jnp.transpose(block) if jb != kb else None
            for n in range(many):
                for p in range(moments):
                    which = (start + n) * moments + p
                    for r in range(2):
                        lane = (2 * p + r) * JB
                        tile, spot = divmod(r * nvec + kb * JB, LANES)
                        full[
                            which * tall + tile, jb * JB : (jb + 1) * JB, spot : spot + JB
                        ] = block[n * JB : (n + 1) * JB, lane : lane + JB]
                        if jb != kb:
                            tile, spot = divmod(r * nvec + jb * JB, LANES)
                            full[
                                which * tall + tile, kb * JB : (kb + 1) * JB, spot : spot + JB
                            ] = turned[lane : lane + JB, n * JB : (n + 1) * JB]
    wide = 2 * nvec
    tiles = 2 * wide // LANES
    half = nvec // 2
    for which in range(rows * moments):
        parity = []
        for odd in range(2):
            for tile in range(tall):
                line = full[which * tall + tile, pl.ds(odd, half, stride=2), :]
                parity.append(line[:, : min(LANES, wide - tile * LANES)])
        both = jnp.concatenate(parity, axis=1)
        i, p = which // moments, which % moments
        base = i * half * tiles * moments
        for tile in range(tiles):
            out_ref[0, pl.ds(base + tile * moments + p, half, stride=tiles * moments), :] = both[
                :, tile * LANES : (tile + 1) * LANES
            ]


def unpack(packed, rows, moments, nvec):
    times = packed.shape[0]
    lines = nvec * nvec * 2 // LANES
    flat = pl.pallas_call(
        functools.partial(unpack_kernel, rows, moments, nvec),
        out_shape=jax.ShapeDtypeStruct((times, rows * lines * moments, LANES), jnp.float32),
        grid=(times,),
        in_specs=[
            pl.BlockSpec((1,) + packed.shape[1:], lambda t: (t, 0, 0)),
        ],
        out_specs=pl.BlockSpec((1, rows * lines * moments, LANES), lambda t: (t, 0, 0)),
        scratch_shapes=[
            pltpu.VMEM((rows * moments * -(-2 * nvec // LANES), nvec, LANES), jnp.float32)
        ],
        compiler_params=pltpu.CompilerParams(dimension_semantics=("arbitrary",)),
        name="unpack",
    )(packed)
    flat = flat.reshape(times, rows, lines, moments, LANES)
    return jnp.transpose(flat, (0, 1, 3, 2, 4)).reshape(times, rows, moments, lines * LANES)


def body(vectors, momenta, offsets):
    local = vectors[0]
    nvec = local.shape[2]
    rows = nvec // lax.axis_size("space")
    packed = elementals(local, momenta, offsets)
    return unpack(packed, rows, momenta.shape[0], nvec)


def solution(mesh):
    return jax.shard_map(
        body,
        mesh=mesh,
        in_specs=(P("tm", None, None, None, "space"), P(), P()),
        out_specs=P(None, "space", None, None),
        check_vma=False,
    )
```

time: 162 us -> 90.3 us (0.56)
  waiting for transfers between devices: 85.5 us -> 0 us
  Pallas kernels: 53.4 us -> 88.7 us
  between operations: 13.2 us -> 0.01 us
  local copies, waits for them, and re-layouts: 7.46 us -> 1.35 us
    all_gather x4 -> x0, waiting for transfers between devices: 84.7 us -> none  [the longest x1 30.9 us: body(): tail = lax.all_gather(tail, 'tm', axis=0)]
    pallas_call x3 -> x1, Pallas kernels: 45.4 us -> 80.7 us  [elementals(): pl.pallas_call(functools.partial(elementals_kernel, scale, chips, times,...]
    dynamic_slice x2 -> x0, local copies, waits for them, and re-layouts: 3.98 us -> none  [the longest x1 1.99 us: body(): late_rows = lax.dynamic_slice_in_dim(late, mine, rows, 3)]
    slice x2 -> x0, local copies, waits for them, and re-layouts: 2.52 us -> none  [the longest x1 1.9 us: body(): early = lax.all_gather(local[..., :half], 'space', axis=0)]
  transfers between devices with their start and end apart: 4 -> 0, of which waited for: 4 -> 0; matrix products, arithmetic and copies ran while one was open for 3% -> 0% of each run, Pallas kernels for 21% -> 0%
where the time goes in v1:
time: 90.3 us; the launch traced here: 90.1 us
  Pallas kernels  88.7 us (98%)
  local copies, waits for them, and re-layouts  1.35 us (1%)
    pallas_call x1, Pallas kernels, elementals(): pl.pallas_call(functools.partial(elementals_kernel, scale, chips, times,...  80.7 us
    pallas_call x1, Pallas kernels, unpack(): pl.pallas_call(functools.partial(unpack_kernel, rows, moments, nvec), out...  8.04 us

profile of v1, /device:TPU:0, one launch (start us, length us, event | category | flops | bytes accessed | tf_op | source)
XLA Modules:
  0.0 90.1 jit_solution(12889624681617565087)
XLA Ops:
  0.0 1.3 %copy.4.off_ref = s32[8,3]{1,0:T(8,128)} copy(s32[8,3]{0,1:T(4,128)} %param.5) | data formatting | bytes 192 | tf_op args[2]
  1.3 80.7 %elementals.1.refs_0_ = bf16[4,384,768]{2,1,0:T(8,128)(2,1)} custom-call(s32[2,3]{1,0:T(2,128)} %mom_ref.1, s32[8,3]{1,0:T(8,128)} %copy.4.off_ref, bf16[2,3,96,512]{3,2,1,0:T(8,128)(2,1)} %bitcast.6), custom_call_target="tpu_custom_call" | custom-call | tf_op jit(solution)/shard_map/elementals/pallas_call | solution.py:337
  82.1 8.0 %unpack.1 = f32[4,3456,128]{2,1,0:T(8,128)} custom-call(bf16[4,384,768]{2,1,0:T(8,128)(2,1)} %elementals.1.refs_0_), custom_call_target="tpu_custom_call" | custom-call | tf_op jit(solution)/shard_map/unpack/pallas_call | solution.py:427

commit v2 on v1

v2 whole, which is shorter than its diff:
```python
import functools
import math

import jax
import jax.numpy as jnp
from jax import lax
from jax.experimental import pallas as pl
from jax.experimental.pallas import tpu as pltpu
from jax.sharding import PartitionSpec as P

LAT = 64
BRICK = 8
BRICK_Z = 8
JB = 32
SPAN = 2
PARTS = 2
LAG = 1
HOP = 3
LANES = 128


MESH = pl.DeviceIdType.MESH


def fill_phase(phase_ref, half, block, mom_ref, off_ref):
    sites = phase_ref.shape[2]
    moments = mom_ref.shape[0]
    site = lax.broadcasted_iota(jnp.int32, (1, sites), 1)
    coords = [site // (BRICK * BRICK_Z), site // BRICK_Z % BRICK, site % BRICK_Z]
    for p in range(moments):
        product = jnp.zeros((1, sites), jnp.int32)
        for axis in range(3):
            product = product + mom_ref[p, axis] * (coords[axis] + off_ref[block, axis])
        angle = (product % LAT).astype(jnp.float32) * (2.0 * math.pi / LAT)
        phase_ref[half, 2 * p : 2 * p + 1, :] = jnp.cos(angle)
        phase_ref[half, 2 * p + 1 : 2 * p + 2, :] = jnp.sin(angle)


def elementals_kernel(
    scale,
    chips,
    times,
    rows,
    mom_ref,
    off_ref,
    v_ref,
    z_ref,
    other_ref,
    phase_ref,
    rowf_ref,
    x_ref,
    lhs_a,
    lhs_b,
    acc_ref,
    own_ref,
    send_ref,
    take_ref,
    pair_sem,
    send_sem,
    take_sem,
    z_sem,
    up_sem,
    down_sem,
):
    nvec = v_ref.shape[2]
    sites = v_ref.shape[3]
    moments = mom_ref.shape[0]
    nblocks = nvec // JB
    group = 2 * moments * JB
    per_half = sites // LANES
    nchunks = 2 * per_half
    depth = 6 * LANES
    me = lax.axis_index("space")
    z = lax.axis_index("tm")
    core = lax.rem(me, 2)
    chip = me // 2
    mate = chip * 2 + 1 - core
    reach = nblocks // 2 + 1
    wide = reach * group
    pieces = nblocks * chips
    share = rows * JB // PARTS
    steps = nchunks // SPAN

    barrier = pltpu.get_barrier_semaphore()

    def greet(where):
        pl.semaphore_signal(barrier, inc=1, device_id=where, device_id_type=MESH)

    greet({"space": mate})
    for s in range(1, chips):
        greet({"space": lax.rem(chip + s, chips) * 2 + core})

    @pl.when(z > 0)
    def _():
        greet({"tm": z - 1})

    @pl.when(z < times - 1)
    def _():
        greet({"tm": z + 1})

    fill_phase(phase_ref, 0, me, mom_ref, off_ref)
    fill_phase(phase_ref, 1, mate, mom_ref, off_ref)
    ends = jnp.minimum(z, 1) + jnp.minimum(times - 1 - z, 1)
    pl.semaphore_wait(barrier, chips + ends)

    pair = pltpu.make_async_remote_copy(
        src_ref=v_ref,
        dst_ref=other_ref,
        send_sem=pair_sem.at[0],
        recv_sem=pair_sem.at[1],
        device_id={"space": mate},
        device_id_type=MESH,
    )
    pair.start()

    def prepare(half, source):
        def one(index, carry):
            lanes = pl.ds(pl.multiple_of(index * LANES, LANES), LANES)
            chunk = half * per_half + index
            step = chunk // SPAN
            place = pl.multiple_of(lax.rem(chunk, SPAN) * depth, LANES)
            for colour in range(3):
                real_v = source[0, colour, :, lanes].astype(jnp.float32)
                imag_v = source[1, colour, :, lanes].astype(jnp.float32)
                rowf_ref[chunk, colour] = real_v
                rowf_ref[chunk, 3 + colour] = imag_v
                for p in range(moments):
                    cosine = phase_ref[half, pl.ds(2 * p, 1), lanes]
                    sine = phase_ref[half, pl.ds(2 * p + 1, 1), lanes]
                    real_x = (cosine * real_v - sine * imag_v).astype(jnp.bfloat16)
                    imag_x = (cosine * imag_v + sine * real_v).astype(jnp.bfloat16)
                    table = ((real_x, -imag_x), (imag_x, real_x))
                    for r in range(2):
                        for part in range(2):
                            at = (colour * 2 + part) * LANES
                            for n in range(nblocks + reach - 1):
                                kb = n % nblocks
                                base = n * group + (2 * p + r) * JB
                                x_ref[step, base : base + JB, pl.ds(place + at, LANES)] = table[r][
                                    part
                                ][kb * JB : (kb + 1) * JB]
            return carry

        lax.fori_loop(0, per_half, one, 0)

    prepare(0, v_ref)
    pair.wait()
    prepare(1, other_ref)

    def target(s):
        return lax.rem(chip + s + 1, chips)

    def form(lhs, piece, step):
        rows_j = pl.ds(pl.multiple_of(piece // chips * JB, JB), JB)
        row0 = (target(lax.rem(piece, chips)) * 2 + core) * rows
        for n in range(SPAN):
            chunk = step * SPAN + n
            vecs = [
                [
                    rowf_ref[chunk, part * 3 + colour, rows_j, :].astype(jnp.bfloat16)
                    for colour in range(3)
                ]
                for part in range(2)
            ]
            for i in range(rows):
                row = [
                    [
                        jnp.broadcast_to(
                            rowf_ref[chunk, part * 3 + colour, pl.ds(row0 + i, 1), :], (JB, LANES)
                        ).astype(jnp.bfloat16)
                        for colour in range(3)
                    ]
                    for part in range(2)
                ]
                for colour in range(3):
                    a = (colour + 1) % 3
                    b = (colour + 2) % 3
                    real_d = (row[0][a] * vecs[0][b] - row[1][a] * vecs[1][b]) - (
                        row[0][b] * vecs[0][a] - row[1][b] * vecs[1][a]
                    )
                    imag_d = (row[0][a] * vecs[1][b] + row[1][a] * vecs[0][b]) - (
                        row[0][b] * vecs[1][a] + row[1][b] * vecs[0][a]
                    )
                    at = n * depth + colour * 2 * LANES
                    lhs[i * JB : (i + 1) * JB, at : at + LANES] = real_d
                    lhs[i * JB : (i + 1) * JB, at + LANES : at + 2 * LANES] = imag_d

    def product(lhs, piece, step):
        rows_x = pl.ds(pl.multiple_of(piece // chips * group, group), wide)
        return lax.dot_general(
            lhs[...],
            x_ref[step, rows_x, :],
            (((1,), (1,)), ((), ())),
            preferred_element_type=jnp.float32,
        )

    def forward(s, jb):
        return pltpu.make_async_remote_copy(
            src_ref=send_ref.at[jb, s],
            dst_ref=take_ref.at[jb, s],
            send_sem=send_sem.at[jb, s],
            recv_sem=take_sem.at[jb, s],
            device_id={"space": target(s) * 2 + core},
            device_id_type=MESH,
        )

    def climb(t, unit):
        jb, part = divmod(unit, PARTS)
        block = pl.ds(part * share, share)
        return pltpu.make_async_remote_copy(
            src_ref=z_ref.at[t, jb, block],
            dst_ref=z_ref.at[t, jb, block],
            send_sem=up_sem.at[unit, t],
            recv_sem=z_sem.at[unit, t],
            device_id={"tm": z + 1},
            device_id_type=MESH,
        )

    def descend(t, unit):
        jb, part = divmod(unit, PARTS)
        block = pl.ds(part * share, share)
        return pltpu.make_async_remote_copy(
            src_ref=z_ref.at[t, jb, block],
            dst_ref=z_ref.at[t, jb, block],
            send_sem=down_sem.at[unit, t],
            recv_sem=z_sem.at[unit, t],
            device_id={"tm": z - 1},
            device_id_type=MESH,
        )

    def finish(jb):
        for s in range(chips - 1):
            forward(s, jb).wait_recv()
        for part in range(PARTS):
            lo, hi = part * share, (part + 1) * share
            total = own_ref[jb, lo:hi]
            for s in range(chips - 1):
                total = total + take_ref[jb, s, lo:hi].astype(jnp.float32)
            z_ref[z, jb, lo:hi] = (total * scale).astype(jnp.bfloat16)
            unit = jb * PARTS + part

            @pl.when(z < times - 1)
            def _():
                climb(z, unit).start()

            @pl.when(z > 0)
            def _():
                descend(z, unit).start()

    def relay(unit, dist):
        @pl.when(z - dist >= 0)
        def _():
            descend(z - dist, unit).wait_recv()

            @pl.when(z < times - 1)
            def _():
                climb(z - dist, unit).start()

        @pl.when(z + dist < times)
        def _():
            climb(z + dist, unit).wait_recv()

            @pl.when(z > 0)
            def _():
                descend(z + dist, unit).start()

    halves = steps // 2
    plan = {}
    tail = []
    events = []
    for jb in range(nblocks):
        begin = halves * chips * (jb + 1) + LAG
        events.append((begin, finish, (jb,)))
        for part in range(PARTS):
            for dist in range(1, times):
                at = begin + part + HOP * dist
                events.append((at, relay, (jb * PARTS + part, dist)))
    events.sort(key=lambda event: event[0])
    for at, act, operands in events:
        if at < halves * pieces:
            plan.setdefault(at, []).append((act, operands))
        else:
            tail.append((act, operands))

    def one(piece, carry):
        jb = piece // chips
        s = lax.rem(piece, chips)
        for step in range(0, steps, 2):
            form(lhs_b, piece, step + 1)
            first = product(lhs_a, piece, step)
            acc_ref[...] = first if step == 0 else acc_ref[...] + first
            if step + 2 < steps:
                form(lhs_a, piece, step + 2)
            else:
                form(lhs_a, lax.rem(piece + 1, pieces), 0)
            acc_ref[...] += product(lhs_b, piece, step + 1)
            for at, acts in plan.items():
                if at % halves == step // 2:

                    @pl.when(piece == at // halves)
                    def _():
                        for act, operands in acts:
                            act(*operands)

        @pl.when(s < chips - 1)
        def _():
            send_ref[jb, s] = acc_ref[...].astype(jnp.bfloat16)
            forward(s, jb).start()

        @pl.when(s == chips - 1)
        def _():
            own_ref[jb] = acc_ref[...]

        return carry

    form(lhs_a, 0, 0)
    lax.fori_loop(0, pieces, one, 0)
    for act, operands in tail:
        act(*operands)

    for jb in range(nblocks):
        for s in range(chips - 1):
            forward(s, jb).wait_send()
    for unit in range(nblocks * PARTS):
        for t in range(times):

            @pl.when((z < times - 1) & (t <= z))
            def _():
                climb(t, unit).wait_send()

            @pl.when((z > 0) & (t >= z))
            def _():
                descend(t, unit).wait_send()


def elementals(local, momenta, offsets):
    nvec = local.shape[2]
    sites = local.shape[3]
    groups = lax.axis_size("space")
    times = lax.axis_size("tm")
    chips = groups // 2
    rows = nvec // groups
    moments = momenta.shape[0]
    nblocks = nvec // JB
    group = 2 * moments * JB
    reach = nblocks // 2 + 1
    wide = reach * group
    nchunks = 2 * sites // LANES
    depth = 6 * LANES
    tall = rows * JB
    scale = 1.0 / math.sqrt(sites * groups)
    dma = pltpu.SemaphoreType.DMA
    return pl.pallas_call(
        functools.partial(elementals_kernel, scale, chips, times, rows),
        out_shape=jax.ShapeDtypeStruct((times, nblocks, tall, wide), jnp.bfloat16),
        in_specs=[
            pl.BlockSpec(memory_space=pltpu.SMEM),
            pl.BlockSpec(memory_space=pltpu.SMEM),
            pl.BlockSpec(memory_space=pltpu.VMEM),
        ],
        out_specs=pl.BlockSpec(memory_space=pltpu.VMEM),
        scratch_shapes=[
            pltpu.VMEM((2, 3, nvec, sites), jnp.bfloat16),
            pltpu.VMEM((2, 2 * moments, sites), jnp.float32),
            pltpu.VMEM((nchunks, 6, nvec, LANES), jnp.float32),
            pltpu.VMEM(
                (nchunks // SPAN, (nblocks + reach - 1) * group, SPAN * depth), jnp.bfloat16
            ),
            pltpu.VMEM((tall, SPAN * depth), jnp.bfloat16),
            pltpu.VMEM((tall, SPAN * depth), jnp.bfloat16),
            pltpu.VMEM((tall, wide), jnp.float32),
            pltpu.VMEM((nblocks, tall, wide), jnp.float32),
            pltpu.VMEM((nblocks, chips - 1, tall, wide), jnp.bfloat16),
            pltpu.VMEM((nblocks, chips - 1, tall, wide), jnp.bfloat16),
            dma((2,)),
            dma((nblocks, chips - 1)),
            dma((nblocks, chips - 1)),
            dma((nblocks * PARTS, times)),
            dma((nblocks * PARTS, times)),
            dma((nblocks * PARTS, times)),
        ],
        compiler_params=pltpu.CompilerParams(
            collective_id=0, has_side_effects=True, vmem_limit_bytes=60 * 1024 * 1024
        ),
        name="elementals",
    )(momenta, offsets, local)


def unpack_kernel(rows, moments, nvec, *refs):
    nblocks = nvec // JB
    group = 2 * moments * JB
    pack = LANES // JB
    source, out_ref, full = refs
    tall = full.shape[0] // (rows * moments)
    pieces = []
    for jb in range(nblocks):
        for d in range(nblocks // 2 + 1):
            pieces.append((jb, (jb + d) % nblocks, d * group))
    for jb, kb, at in pieces:
        for start in range(0, rows, pack):
            many = min(pack, rows - start)
            block = source[0, jb, start * JB : (start + many) * JB, at : at + group].astype(
                jnp.float32
            )
            turned = -jnp.transpose(block) if jb != kb else None
            for n in range(many):
                for p in range(moments):
                    which = (start + n) * moments + p
                    for r in range(2):
                        lane = (2 * p + r) * JB
                        tile, spot = divmod(r * nvec + kb * JB, LANES)
                        full[
                            which * tall + tile, jb * JB : (jb + 1) * JB, spot : spot + JB
                        ] = block[n * JB : (n + 1) * JB, lane : lane + JB]
                        if jb != kb:
                            tile, spot = divmod(r * nvec + jb * JB, LANES)
                            full[
                                which * tall + tile, kb * JB : (kb + 1) * JB, spot : spot + JB
                            ] = turned[lane : lane + JB, n * JB : (n + 1) * JB]
    wide = 2 * nvec
    tiles = 2 * wide // LANES
    half = nvec // 2
    for which in range(rows * moments):
        parity = []
        for odd in range(2):
            for tile in range(tall):
                line = full[which * tall + tile, pl.ds(odd, half, stride=2), :]
                parity.append(line[:, : min(LANES, wide - tile * LANES)])
        both = jnp.concatenate(parity, axis=1)
        i, p = which // moments, which % moments
        base = i * half * tiles * moments
        for tile in range(tiles):
            out_ref[0, pl.ds(base + tile * moments + p, half, stride=tiles * moments), :] = both[
                :, tile * LANES : (tile + 1) * LANES
            ]


def unpack(packed, rows, moments, nvec):
    times = packed.shape[0]
    lines = nvec * nvec * 2 // LANES
    flat = pl.pallas_call(
        functools.partial(unpack_kernel, rows, moments, nvec),
        out_shape=jax.ShapeDtypeStruct((times, rows * lines * moments, LANES), jnp.float32),
        grid=(times,),
        in_specs=[
            pl.BlockSpec((1,) + packed.shape[1:], lambda t: (t, 0, 0, 0)),
        ],
        out_specs=pl.BlockSpec((1, rows * lines * moments, LANES), lambda t: (t, 0, 0)),
        scratch_shapes=[
            pltpu.VMEM((rows * moments * -(-2 * nvec // LANES), nvec, LANES), jnp.float32)
        ],
        compiler_params=pltpu.CompilerParams(dimension_semantics=("arbitrary",)),
        name="unpack",
    )(packed)
    flat = flat.reshape(times, rows, lines, moments, LANES)
    return jnp.transpose(flat, (0, 1, 3, 2, 4)).reshape(times, rows, moments, lines * LANES)


def body(vectors, momenta, offsets):
    local = vectors[0]
    nvec = local.shape[2]
    rows = nvec // lax.axis_size("space")
    packed = elementals(local, momenta, offsets)
    return unpack(packed, rows, momenta.shape[0], nvec)


def solution(mesh):
    return jax.shard_map(
        body,
        mesh=mesh,
        in_specs=(P("tm", None, None, None, "space"), P(), P()),
        out_specs=P(None, "space", None, None),
        check_vma=False,
    )
```

time: 90.3 us -> 77.6 us (0.86)
  Pallas kernels: 88.7 us -> 76 us
    pallas_call x1, Pallas kernels: 80.7 us -> 68 us  [elementals(): pl.pallas_call(functools.partial(elementals_kernel, scale, chips, times,...]
where the time goes in v2:
time: 77.6 us; the launch traced here: 77.3 us
  Pallas kernels  76 us (98%)
  local copies, waits for them, and re-layouts  1.35 us (2%)
    pallas_call x1, Pallas kernels, elementals(): pl.pallas_call(functools.partial(elementals_kernel, scale, chips, times,...  68 us
    pallas_call x1, Pallas kernels, unpack(): pl.pallas_call(functools.partial(unpack_kernel, rows, moments, nvec), out...  7.92 us

profile of v2, /device:TPU:0, one launch (start us, length us, event | category | flops | bytes accessed | tf_op | source)
XLA Modules:
  0.0 77.3 jit_solution(13370293889058933326)
XLA Ops:
  0.0 1.3 %copy.4.off_ref = s32[8,3]{1,0:T(8,128)} copy(s32[8,3]{0,1:T(4,128)} %param.5) | data formatting | bytes 192 | tf_op args[2]
  1.3 68.0 %elementals.1.refs_0_ = bf16[4,3,384,256]{3,2,1,0:T(8,128)(2,1)} custom-call(s32[2,3]{1,0:T(2,128)} %mom_ref.1, s32[8,3]{1,0:T(8,128)} %copy.4.off_ref, bf16[2,3,96,512]{3,2,1,0:T(8,128)(2,1)} %bitcast.6), custom_call_target="tpu_custom_call" | custom-call | tf_op jit(solution)/shard_map/elementals/pallas_call | solution.py:353
  69.4 7.9 %unpack.1 = f32[4,3456,128]{2,1,0:T(8,128)} custom-call(bf16[4,3,384,256]{3,2,1,0:T(8,128)(2,1)} %elementals.1.refs_0_), custom_call_target="tpu_custom_call" | custom-call | tf_op jit(solution)/shard_map/unpack/pallas_call | solution.py:441

commit v3 on v2

--- a/solution.py
+++ b/solution.py
@@ -12,10 +12,10 @@
 BRICK = 8
 BRICK_Z = 8
 JB = 32
-SPAN = 2
+SPAN = 4
 PARTS = 2
 LAG = 1
-HOP = 3
+HOP = 2
 LANES = 128
 
 
@@ -30,10 +30,21 @@
     for p in range(moments):
         product = jnp.zeros((1, sites), jnp.int32)
         for axis in range(3):
-            product = product + mom_ref[p, axis] * (coords[axis] + off_ref[block, axis])
+            product = product + mom_ref[p, axis] * (coords[axis] + off_ref[axis, block])
         angle = (product % LAT).astype(jnp.float32) * (2.0 * math.pi / LAT)
         phase_ref[half, 2 * p : 2 * p + 1, :] = jnp.cos(angle)
         phase_ref[half, 2 * p + 1 : 2 * p + 2, :] = jnp.sin(angle)
+
+
+def spots(height, width):
+    j = lax.broadcasted_iota(jnp.int32, (height, width), 0) % (JB // 2)
+    k = lax.broadcasted_iota(jnp.int32, (height, width), 1) % JB
+    return j, k
+
+
+def folded(height, width):
+    j, k = spots(height, width)
+    return k > j
 
 
 def elementals_kernel(
@@ -79,6 +90,7 @@
     wide = reach * group
     pieces = nblocks * chips
     share = rows * JB // PARTS
+    slab = share * reach - share // 2
     steps = nchunks // SPAN
 
     barrier = pltpu.get_barrier_semaphore()
@@ -206,7 +218,7 @@
 
     def climb(t, unit):
         jb, part = divmod(unit, PARTS)
-        block = pl.ds(part * share, share)
+        block = pl.ds(part * slab, slab)
         return pltpu.make_async_remote_copy(
             src_ref=z_ref.at[t, jb, block],
             dst_ref=z_ref.at[t, jb, block],
@@ -218,7 +230,7 @@
 
     def descend(t, unit):
         jb, part = divmod(unit, PARTS)
-        block = pl.ds(part * share, share)
+        block = pl.ds(part * slab, slab)
         return pltpu.make_async_remote_copy(
             src_ref=z_ref.at[t, jb, block],
             dst_ref=z_ref.at[t, jb, block],
@@ -236,7 +248,20 @@
             total = own_ref[jb, lo:hi]
             for s in range(chips - 1):
                 total = total + take_ref[jb, s, lo:hi].astype(jnp.float32)
-            z_ref[z, jb, lo:hi] = (total * scale).astype(jnp.bfloat16)
+            total = total * scale
+            at = part * slab
+            for d in range(1, reach):
+                z_ref[z, jb, at : at + share] = total[:, d * group : (d + 1) * group].astype(
+                    jnp.bfloat16
+                )
+                at += share
+            square = total[:, :group].reshape(share // JB, JB, group)
+            upper = square[:, : JB // 2].reshape(share // 2, group)
+            lower = square[:, JB // 2 :].reshape(share // 2, group)
+            keep = folded(share // 2, group)
+            z_ref[z, jb, at : at + share // 2] = jnp.where(
+                keep, upper, pltpu.roll(lower, group - JB // 2, 1)
+            ).astype(jnp.bfloat16)
             unit = jb * PARTS + part
 
             @pl.when(z < times - 1)
@@ -352,7 +377,9 @@
     dma = pltpu.SemaphoreType.DMA
     return pl.pallas_call(
         functools.partial(elementals_kernel, scale, chips, times, rows),
-        out_shape=jax.ShapeDtypeStruct((times, nblocks, tall, wide), jnp.bfloat16),
+        out_shape=jax.ShapeDtypeStruct(
+            (times, nblocks, tall * reach - tall // 2, group), jnp.bfloat16
+        ),
         in_specs=[
             pl.BlockSpec(memory_space=pltpu.SMEM),
             pl.BlockSpec(memory_space=pltpu.SMEM),
@@ -383,56 +410,119 @@
             collective_id=0, has_side_effects=True, vmem_limit_bytes=60 * 1024 * 1024
         ),
         name="elementals",
-    )(momenta, offsets, local)
-
-
-def unpack_kernel(rows, moments, nvec, *refs):
+    )(momenta, jnp.transpose(offsets), local)
+
+
+def unpack_kernel(rows, moments, nvec, source, out_ref, grid_ref, place_ref, near_ref, far_ref):
     nblocks = nvec // JB
     group = 2 * moments * JB
     pack = LANES // JB
-    source, out_ref, full = refs
-    tall = full.shape[0] // (rows * moments)
-    pieces = []
-    for jb in range(nblocks):
-        for d in range(nblocks // 2 + 1):
-            pieces.append((jb, (jb + d) % nblocks, d * group))
-    for jb, kb, at in pieces:
-        for start in range(0, rows, pack):
-            many = min(pack, rows - start)
-            block = source[0, jb, start * JB : (start + many) * JB, at : at + group].astype(
-                jnp.float32
-            )
-            turned = -jnp.transpose(block) if jb != kb else None
-            for n in range(many):
-                for p in range(moments):
-                    which = (start + n) * moments + p
-                    for r in range(2):
-                        lane = (2 * p + r) * JB
-                        tile, spot = divmod(r * nvec + kb * JB, LANES)
-                        full[
-                            which * tall + tile, jb * JB : (jb + 1) * JB, spot : spot + JB
-                        ] = block[n * JB : (n + 1) * JB, lane : lane + JB]
-                        if jb != kb:
-                            tile, spot = divmod(r * nvec + jb * JB, LANES)
-                            full[
-                                which * tall + tile, kb * JB : (kb + 1) * JB, spot : spot + JB
-                            ] = turned[lane : lane + JB, n * JB : (n + 1) * JB]
     wide = 2 * nvec
     tiles = 2 * wide // LANES
-    half = nvec // 2
-    for which in range(rows * moments):
-        parity = []
+    starts = (0, wide // LANES)
+    counts = (-(-wide // LANES), tiles - wide // LANES)
+
+    @pl.when(pl.program_id(0) == 0)
+    def _():
         for odd in range(2):
-            for tile in range(tall):
-                line = full[which * tall + tile, pl.ds(odd, half, stride=2), :]
-                parity.append(line[:, : min(LANES, wide - tile * LANES)])
-        both = jnp.concatenate(parity, axis=1)
-        i, p = which // moments, which % moments
-        base = i * half * tiles * moments
+            span = counts[odd] * LANES
+            shape = (group, moments * span)
+            lane = lax.broadcasted_iota(jnp.int32, shape, 0)
+            col = lax.broadcasted_iota(jnp.int32, shape, 1)
+            which, k = lane // JB, lane % JB
+            for kb in range(nblocks):
+                goal = which % 2 * nvec + kb * JB + k + odd * wide - starts[odd] * LANES
+                hit = which // 2 * span + goal == col
+                place_ref[odd, kb * group : (kb + 1) * group, : moments * span] = jnp.where(
+                    hit, 1.0, 0.0
+                ).astype(jnp.bfloat16)
+
+    reach = nblocks // 2 + 1
+    small = JB // 2
+    per = rows // PARTS
+    slab = per * (reach * JB - small)
+
+    def spot(i, d):
+        part, n = divmod(i, per)
+        if d == 0:
+            return part * slab + per * (reach - 1) * JB + n * small
+        return part * slab + (per * (d - 1) + n) * JB
+
+    def take(jb, start, many, d):
+        tall = small if d == 0 else JB
+        return jnp.concatenate(
+            [
+                source[0, jb, spot(start + n, d) : spot(start + n, d) + tall, :].astype(jnp.float32)
+                for n in range(many)
+            ],
+            axis=0,
+        )
+
+    for jb in range(nblocks):
+        for d in range(1, reach):
+            kb = (jb + d) % nblocks
+            for start in range(0, rows, pack):
+                many = min(pack, rows - start)
+                block = take(jb, start, many, d)
+                turned = -jnp.transpose(block)
+                for n in range(many):
+                    base = (start + n) * nvec
+                    grid_ref[kb, base + jb * JB : base + (jb + 1) * JB, :] = block[
+                        n * JB : (n + 1) * JB, :
+                    ]
+                    for which in range(2 * moments):
+                        grid_ref[
+                            jb, base + kb * JB : base + (kb + 1) * JB, which * JB : (which + 1) * JB
+                        ] = turned[which * JB : (which + 1) * JB, n * JB : (n + 1) * JB]
+        for start in range(0, rows, 2 * pack):
+            many = min(2 * pack, rows - start)
+            block = take(jb, start, many, 0)
+            turned = -jnp.transpose(block)
+            for n in range(many):
+                for which in range(2 * moments):
+                    lane = which * JB
+                    near = turned[lane : lane + small, n * small : (n + 1) * small]
+                    far = turned[lane + small : lane + JB, n * small : (n + 1) * small]
+                    near_ref[n * small : (n + 1) * small, lane : lane + small] = near
+                    near_ref[n * small : (n + 1) * small, lane + small : lane + JB] = near
+                    far_ref[n * small : (n + 1) * small, lane : lane + small] = far
+            height = many * small
+            j, k = spots(height, group)
+            near = near_ref[:height, :]
+            top = jnp.where(k > j, block, jnp.where(k < j, near, 0.0))
+            lag = k - small
+            moved = pltpu.roll(block, small, 1)
+            low = jnp.where(lag < j, moved, jnp.where(lag > j, near, 0.0))
+            low = jnp.where(k < small, far_ref[:height, :], low)
+            for n in range(many):
+                base = (start + n) * nvec + jb * JB
+                grid_ref[jb, base : base + small, :] = top[n * small : (n + 1) * small, :]
+                grid_ref[jb, base + small : base + JB, :] = low[n * small : (n + 1) * small, :]
+    lines = rows * nvec // 2
+    moved = []
+    for odd in range(2):
+        taken = [
+            grid_ref[kb, pl.ds(odd, lines, stride=2), :].astype(jnp.bfloat16)
+            for kb in range(nblocks)
+        ]
+        moved.append(
+            jnp.dot(
+                jnp.concatenate(taken, axis=1),
+                place_ref[odd, :, : moments * counts[odd] * LANES],
+                preferred_element_type=jnp.float32,
+            )
+        )
+    for p in range(moments):
         for tile in range(tiles):
-            out_ref[0, pl.ds(base + tile * moments + p, half, stride=tiles * moments), :] = both[
-                :, tile * LANES : (tile + 1) * LANES
-            ]
+            parts = []
+            for odd in range(2):
+                n = tile - starts[odd]
+                if 0 <= n < counts[odd]:
+                    at = (p * counts[odd] + n) * LANES
+                    parts.append(moved[odd][:, at : at + LANES])
+            out_ref[0, pl.ds(tile * moments + p, lines, stride=tiles * moments), :] = sum(
+                parts[1:], parts[0]
+            )
 
 
 def unpack(packed, rows, moments, nvec):
@@ -447,7 +537,12 @@
         ],
         out_specs=pl.BlockSpec((1, rows * lines * moments, LANES), lambda t: (t, 0, 0)),
         scratch_shapes=[
-            pltpu.VMEM((rows * moments * -(-2 * nvec // LANES), nvec, LANES), jnp.float32)
+            pltpu.VMEM((nvec // JB, rows * nvec, LANES), jnp.float32),
+            pltpu.VMEM(
+                (2, nvec // JB * LANES, moments * -(-2 * nvec // LANES) * LANES), jnp.bfloat16
+            ),
+            pltpu.VMEM((LANES, LANES), jnp.float32),
+            pltpu.VMEM((LANES, LANES), jnp.float32),
         ],
         compiler_params=pltpu.CompilerParams(dimension_semantics=("arbitrary",)),
         name="unpack",

time: 77.6 us -> 73.5 us (0.947)
  Pallas kernels: 76 us -> 73.3 us
  local copies, waits for them, and re-layouts: 1.35 us -> 0 us
    pallas_call x1, Pallas kernels: 68 us -> 62.7 us  [elementals(): pl.pallas_call(functools.partial(elementals_kernel, scale, chips, times,...]
    pallas_call x1, Pallas kernels: 7.92 us -> 10.6 us  [unpack(): pl.pallas_call(functools.partial(unpack_kernel, rows, moments, nvec), out...]
    unnamed x1 -> x0, local copies, waits for them, and re-layouts: 1.35 us -> none
where the time goes in v3:
time: 73.5 us; the launch traced here: 73.3 us
  Pallas kernels  73.3 us (100%)
    pallas_call x1, Pallas kernels, elementals(): pl.pallas_call(functools.partial(elementals_kernel, scale, chips, times,...  62.7 us
    pallas_call x1, Pallas kernels, unpack(): pl.pallas_call(functools.partial(unpack_kernel, rows, moments, nvec), out...  10.6 us

profile of v3, /device:TPU:0, one launch (start us, length us, event | category | flops | bytes accessed | tf_op | source)
XLA Modules:
  0.0 73.3 jit_solution(16755530750792634294)
XLA Ops:
  0.0 62.7 %elementals.1.source = bf16[4,3,576,128]{3,2,1,0:T(8,128)(2,1)} custom-call(s32[2,3]{1,0:T(2,128)} %mom_ref.1, s32[3,8]{1,0:T(4,128)} %bitcast.8, bf16[2,3,96,512]{3,2,1,0:T(8,128)(2,1)} %bitcast.7), custom_call_target="tpu_custom_call" | custom-call | tf_op jit(solution)/shard_map/elementals/pallas_call | solution.py:378
  62.7 10.6 %unpack.1 = f32[4,3456,128]{2,1,0:T(8,128)} custom-call(bf16[4,3,576,128]{3,2,1,0:T(8,128)(2,1)} %elementals.1.source), custom_call_target="tpu_custom_call" | custom-call | tf_op jit(solution)/shard_map/unpack/pallas_call | solution.py:531
